TPU v7x, 32 devices: a whole 2x2x4 slice. The times are simulated.
32 devices in a mesh: replica: 8 (over z, core), tp: 4 (over y, x).
Axes of the slice: x: 2, y: 2, z: 4, core: 2. Of those that a mesh axis runs over, the one named last changes fastest.
Arguments:
- token_ids: int32 [128], replicated, may hold values from 0 to 8191
- embed_table: bfloat16 [8192, 8192], P('replica', 'tp'), may hold values from -6 to 6
- norm_gain: bfloat16 [8192], replicated, may hold values from 0.099609375 to 1.8984375
- w_query: bfloat16 [8192, 4096], P(('replica', 'tp')), may hold values from -0.0625 to 0.0625
- w_keyvalue: bfloat16 [8192, 2, 512], P(('replica', 'tp')), may hold values from -0.0625 to 0.0625
- key_cache: bfloat16 [512, 1024, 128], P(('replica', 'tp')), may hold values from -360 to 360
- value_cache: bfloat16 [512, 1024, 128], P(('replica', 'tp')), may hold values from -6 to 6
- cache_lengths: int32 [128], P('replica'), may hold values from 1 to 1024, as said below
Outputs:
- context: bfloat16 [512, 1024], P(('replica', 'tp'))
- query_weight_tp: bfloat16 [8192, 4096], P(None, 'tp')
- keyvalue_weight_tp: bfloat16 [8192, 2, 512], P(None, None, 'tp')
Inputs may be any that keep to these rules, and one draw needn't show every extreme that they name: `cache_lengths`: some sequence has exactly 1024 filled slots.
All inputs are finite; a program needn't handle non-finite values.
Results may differ from a plain program's by a relative error of at most 0.019.
The roundings to bfloat16 on the way count: a program that leaves them out, or rounds other values in their place, can miss the bound.
Values may be sent and summed in bfloat16 or wider, within the bound.
A program may use at most 128 MiB of HBM per device.

v0:
```python
import jax
import jax.numpy as jnp
from jax import lax
from jax.sharding import PartitionSpec as P


def attend(query, keys, values, key_new, value_new, lengths):
    scale = query.shape[-1] ** (-0.5)
    scores = jnp.einsum("rgd,rcd->rgc", query, keys, preferred_element_type=jnp.float32) * scale
    position = lax.broadcasted_iota(jnp.int32, scores.shape, 2)
    scores = jnp.where(position < lengths[:, None, None], scores, -jnp.inf)
    own = jnp.einsum("rgd,rd->rg", query, key_new, preferred_element_type=jnp.float32) * scale
    top = jnp.maximum(jnp.max(scores, axis=2), own)
    weights = jnp.exp(scores - top[:, :, None])
    own_weight = jnp.exp(own - top)
    total = jnp.sum(weights, axis=2) + own_weight
    weights = (weights / total[:, :, None]).astype(jnp.bfloat16)
    own_weight = (own_weight / total).astype(jnp.bfloat16)
    context = jnp.einsum("rgc,rcd->rgd", weights, values, preferred_element_type=jnp.float32)
    context = (
        context
        + own_weight.astype(jnp.float32)[:, :, None] * value_new.astype(jnp.float32)[:, None, :]
    )
    return context.astype(jnp.bfloat16)


def per_device(
    token_ids, embed_table, norm_gain, w_query, w_keyvalue, key_cache, value_cache, cache_lengths
):
    group_index = lax.axis_index("replica")
    tp_index = lax.axis_index("tp")
    vocab_rows, feature_cols = embed_table.shape
    batch = cache_lengths.shape[0]
    first_id = group_index * vocab_rows
    picked = token_ids - first_id
    columns = lax.broadcasted_iota(jnp.int32, (batch * lax.axis_size("replica"), vocab_rows), 1)
    onehot = (picked[:, None] == columns).astype(jnp.bfloat16)
    embedded = lax.psum_scatter(
        jnp.dot(onehot, embed_table, preferred_element_type=jnp.float32),
        "replica",
        scatter_dimension=0,
        tiled=True,
    ).astype(jnp.bfloat16)
    whole = lax.all_gather(embedded, "tp", axis=1, tiled=True)
    values32 = whole.astype(jnp.float32)
    mean_square = jnp.mean(values32 * values32, axis=1, keepdims=True)
    normed = (values32 * lax.rsqrt(mean_square + 1e-05) * norm_gain.astype(jnp.float32)).astype(
        jnp.bfloat16
    )
    width = normed.shape[1]
    query_rows = w_query.reshape(w_query.shape[0], 1, w_query.shape[1])
    query_mid, pair_mid = (
        lax.all_to_all(query_rows, "tp", split_axis=2, concat_axis=0, tiled=True),
        lax.all_to_all(w_keyvalue, "tp", split_axis=2, concat_axis=0, tiled=True),
    )
    flat_query = query_mid.reshape(query_mid.shape[0], query_mid.shape[2])
    pair_cols = pair_mid.shape[2]
    flat_pair = pair_mid.reshape(pair_mid.shape[0], 2 * pair_cols)
    query_full, pair_full = (
        lax.all_gather(flat_query, "replica", axis=0, tiled=True),
        lax.all_gather(flat_pair, "replica", axis=0, tiled=True),
    )
    query_acc = jnp.dot(normed, query_full, preferred_element_type=jnp.float32)
    pair_acc = jnp.dot(normed, pair_full, preferred_element_type=jnp.float32)
    query_local = query_acc.astype(jnp.bfloat16)
    pair_local = pair_acc.astype(jnp.bfloat16).reshape(batch, 2, pair_cols)
    query_heads, pair_heads = (
        lax.all_gather(query_local, "tp", axis=1, tiled=True),
        lax.all_gather(pair_local, "tp", axis=2, tiled=True),
    )
    head_size = key_cache.shape[2]
    kv_heads = pair_heads.shape[2] // head_size
    group = query_heads.shape[1] // (kv_heads * head_size)
    rows_here = key_cache.shape[0]
    first_row = tp_index * rows_here
    query_grouped = (
        query_heads.reshape(batch, kv_heads, group, head_size)
        .transpose(1, 0, 2, 3)
        .reshape(kv_heads * batch, group, head_size)
    )
    key_grouped = (
        pair_heads[:, 0]
        .reshape(batch, kv_heads, head_size)
        .transpose(1, 0, 2)
        .reshape(kv_heads * batch, head_size)
    )
    value_grouped = (
        pair_heads[:, 1]
        .reshape(batch, kv_heads, head_size)
        .transpose(1, 0, 2)
        .reshape(kv_heads * batch, head_size)
    )
    query_mine = lax.dynamic_slice_in_dim(query_grouped, first_row, rows_here, 0)
    key_mine = lax.dynamic_slice_in_dim(key_grouped, first_row, rows_here, 0)
    value_mine = lax.dynamic_slice_in_dim(value_grouped, first_row, rows_here, 0)
    sequence = (first_row + lax.broadcasted_iota(jnp.int32, (rows_here,), 0)) % batch
    matches = sequence[:, None] == lax.broadcasted_iota(jnp.int32, (rows_here, batch), 1)
    row_lengths = jnp.sum(jnp.where(matches, cache_lengths[None, :], 0), axis=1)
    context = attend(query_mine, key_cache, value_cache, key_mine, value_mine, row_lengths)
    context = context.reshape(rows_here, group * head_size)
    return (context, query_full, pair_full.reshape(width, 2, pair_cols))


def solution(mesh):
    return jax.shard_map(
        per_device,
        mesh=mesh,
        in_specs=(
            P(),
            P("replica", "tp"),
            P(),
            P(("replica", "tp"), None),
            P(("replica", "tp"), None, None),
            P(("replica", "tp"), None, None),
            P(("replica", "tp"), None, None),
            P("replica"),
        ),
        out_specs=(P(("replica", "tp"), None), P(None, "tp"), P(None, None, "tp")),
        check_vma=False,
    )
```

profile of v0, /device:TPU:0, one launch (start us, length us, event | category | flops | bytes accessed | tf_op | source)
XLA Modules:
  0.0 279.0 jit_solution(18418797829905342189)
XLA Ops:
  7.2 0.0 copy-start.3
  7.2 0.0 reduce-scatter.2.cloned.1.call-start
  7.2 0.7 broadcast_subtract_fusion
  7.9 3.9 %fusion.6 = f32[128,2048]{1,0:T(8,128)} fusion(bf16[1024,2048]{1,0:T(8,128)(2,1)} %param.9, s32[128]{0:T(128)S(1)} %broadcast_subtract_fusion), kind=kOutput, calls=%fused_computation.17 | convolution fusion | flops 537001984 | bytes 5243392 | tf_op jit(solution)/shard_map/dot_general | solution.py:39
  11.9 0.0 reduce-scatter.2.cloned.1.call-update
  11.9 0.0 all-gather.5.cloned.1.call-start
  11.9 0.0 copy-done.3
  11.9 1.0 copy.59
  12.9 13.5 %all_to_all.30 = bf16[256,2,512]{0,1,2:T(2,128)(2,1)S(1)} all-to-all(bf16[256,2,512]{0,1,2:T(2,128)(2,1)S(1)} %copy.59), channel_id=1, replica_groups=mesh['replica'=8,'tp'=4] {'tp'}, dimensions={2} | all-to-all | bytes 1048576 | tf_op jit(solution)/shard_map/all_to_all | solution.py:54
  26.5 0.6 copy.60
  27.1 0.9 copy.76
  28.0 0.0 all-gather.5.cloned.1.call-update
  28.0 0.0 all-gather.3.cloned.1.call-start
  28.1 0.0 copy-done.2
  28.1 7.1 %copy.56 = bf16[256,1,4096]{0,1,2:T(2,128)(2,1)} copy(bf16[256,1,4096]{2,0,1:T(8,128)(2,1)S(1)} %bitcast.52) | data formatting | bytes 4194304 | tf_op jit(solution)/shard_map/reshape | solution.py:51
  35.1 0.5 broadcast.60
  35.6 21.6 %reduce = bf16[4096,256]{1,0:T(8,128)(2,1)S(1)} reduce(bf16[4096,1,256]{2,1,0:T(2,128)(2,1)} %bitcast.48, bf16[]{:T(256)} %broadcast.60), dimensions={1}, to_apply=%bitcast.36.reduce_sub_computation | reduce | bytes 4194306
  57.2 2.1 reshape.81
  59.3 27.9 %all_to_all.31 = bf16[4,2,131072]{2,1,0:T(2,128)(2,1)S(1)} all-to-all(bf16[4,2,131072]{2,1,0:T(2,128)(2,1)} %reshape.81), channel_id=1, replica_groups=mesh['replica'=8,'tp'=4] {'tp'}, dimensions={0} | all-to-all | bytes 4194304 | tf_op jit(solution)/shard_map/all_to_all | solution.py:53
  87.1 3.3 %reshape.82 = bf16[4096,1,256]{2,1,0:T(2,128)(2,1)} reshape(bf16[4,2,131072]{2,1,0:T(2,128)(2,1)S(1)} %all_to_all.31) | data formatting | bytes 4194304
  90.4 2.6 copy.66
  93.0 0.0 copy-start.4
  93.0 0.0 copy-start.5
  93.0 2.4 copy.57
  95.4 0.0 all-gather.3.cloned.1.call-update
  95.4 0.0 copy-done.4
  95.5 0.2 select_reduce_fusion
  95.7 0.0 reduce-scatter.2.cloned.1.call-done
  95.7 0.9 convert_element_type.34
  96.6 8.4 %all_gather.15 = bf16[16,8192]{1,0:T(8,128)(2,1)S(1)} all-gather(bf16[16,2048]{1,0:T(8,128)(2,1)S(1)} %convert_element_type.34), channel_id=1, replica_groups=mesh['replica'=8,'tp'=4] {'tp'}, dimensions={1}, use_global_device_ids=true | all-gather | bytes 327680 | tf_op jit(solution)/shard_map/all_gather | solution.py:44
  105.0 0.2 fusion.3
  105.2 0.0 all-gather.5.cloned.1.call-done
  105.2 3.8 %fusion.2 = bf16[2,2,8,128]{3,2,1,0:T(8,128)(2,1)S(1)} fusion(bf16[8192,256]{1,0:T(8,128)(2,1)} %all-gather.5.cloned.1.call-done, bf16[16,8192]{1,0:T(8,128)(2,1)S(1)} %all_gather.15, f32[8192]{0:T(1024)S(1)} %convert_element_type.36, f32[16]{0:T(128)S(1)} %add_rsqrt_fusion), kind=kOutput, calls=%fused_computation.6 | convolution fusion | flops 67637248 | bytes 4497472 | tf_op jit(solution)/shard_map/dot_general | solution.py:64
  109.0 7.4 %all_gather.19 = bf16[16,2,512]{2,0,1:T(8,128)(2,1)S(1)} all-gather(bf16[16,2,128]{2,0,1:T(8,128)(2,1)S(1)} %bitcast.65), channel_id=1, replica_groups=mesh['replica'=8,'tp'=4] {'tp'}, dimensions={2}, use_global_device_ids=true | all-gather | bytes 40960 | tf_op jit(solution)/shard_map/all_gather | solution.py:69
  116.5 7.0 %reshape.78 = bf16[8192,2,128]{2,1,0:T(2,128)(2,1)} reshape(bf16[8192,256]{1,0:T(8,128)(2,1)} %all-gather.5.cloned.1.call-done) | data formatting | bytes 8388608 | tf_op jit(solution)/shard_map/reshape | solution.py:101
  123.5 122.8 %all-gather.3.cloned.1.call-done = bf16[8192,1024]{1,0:T(8,128)(2,1)} async-done(((bf16[1024,1024]{1,0:T(8,128)(2,1)}), bf16[8192,1024]{1,0:T(8,128)(2,1)}) %all-gather.3.cloned.1.call-update) | async-done | bytes 16777232 | tf_op jit(solution)/shard_map/all_gather | solution.py:60
  246.3 8.2 %convolution_convert_fusion = bf16[16,1024]{1,0:T(8,128)(2,1)S(1)} fusion(bf16[8192,1024]{1,0:T(8,128)(2,1)} %all-gather.3.cloned.1.call-done, bf16[16,8192]{1,0:T(8,128)(2,1)S(1)} %all_gather.15, f32[8192]{0:T(1024)S(1)} %convert_element_type.36, f32[16]{0:T(128)S(1)} %add_rsqrt_fusion), kind=kOutput, calls=%fused_computation.4 | convolution fusion | flops 268976128 | bytes 17104960 | tf_op jit(solution)/shard_map/dot_general | solution.py:63
  254.5 8.7 %all_gather.17 = bf16[16,4096]{1,0:T(8,128)(2,1)S(1)} all-gather(bf16[16,1024]{1,0:T(8,128)(2,1)S(1)} %convolution_convert_fusion), channel_id=1, replica_groups=mesh['replica'=8,'tp'=4] {'tp'}, dimensions={1}, use_global_device_ids=true | all-gather | bytes 163840 | tf_op jit(solution)/shard_map/all_gather | solution.py:68
  263.3 0.1 fusion.13
  263.4 0.0 slice-start.3
  263.4 1.3 fusion.23
  264.7 0.2 fusion.7
  264.9 0.0 copy-done
  265.0 0.7 fusion.1
  265.7 0.6 copy.77
  266.3 0.0 slice-done.1
  266.3 0.0 slice-done.3
  266.3 6.2 %copy.80 = bf16[8192,1024]{1,0:T(8,128)(2,1)} copy(bf16[8192,1024]{1,0:T(8,128)(2,1)S(1)} %bitcast.47) | data formatting | bytes 33554432
  (26 shorter events, 0.2 us)
Async XLA Ops:
  7.2 4.8 %copy-start.3 = (bf16[256,2,512]{2,1,0:T(2,128)(2,1)S(1)}, bf16[256,2,512]{2,1,0:T(2,128)(2,1)}, u32[]{:S(2)}) copy-start(bf16[256,2,512]{2,1,0:T(2,128)(2,1)} %param.12) | copy-start | bytes 1572868
  7.2 88.5 %reduce-scatter.2.cloned.1.call-start = ((), (), s32[]{:S(2)}) async-start(), calls=%async_computation.3 | async-start | bytes 1179648 | tf_op jit(solution)/shard_map/reduce_scatter | solution.py:38
  11.8 16.2 %copy-start.2 = (bf16[256,4096]{1,0:T(8,128)(2,1)S(1)}, bf16[256,4096]{1,0:T(8,128)(2,1)}, u32[]{:S(2)}) copy-start(bf16[256,4096]{1,0:T(8,128)(2,1)} %param.11) | copy-start | bytes 6291460
  11.9 93.3 %all-gather.5.cloned.1.call-start = ((), (), s32[]{:S(2)}) async-start(), calls=%async_computation.5 | async-start | bytes 4718592 | tf_op jit(solution)/shard_map/all_gather | solution.py:61
  28.0 218.3 %all-gather.3.cloned.1.call-start = ((), (), s32[]{:S(2)}) async-start(), calls=%async_computation.4 | async-start | bytes 18874368 | tf_op jit(solution)/shard_map/all_gather | solution.py:60
  93.0 2.4 copy-start.4
  93.0 2.5 copy-start.5
  246.3 17.1 %copy-start.1 = (bf16[16,1024,128]{2,1,0:T(8,128)(2,1)S(1)}, bf16[16,1024,128]{2,1,0:T(8,128)(2,1)}, u32[]{:S(2)}) copy-start(bf16[16,1024,128]{2,1,0:T(8,128)(2,1)} %param.13) | copy-start | bytes 12582916
  246.3 20.0 %slice-start = ((s8[16777216]{0:T(1024)(128)(4,1)}), s8[4194304]{0:T(1024)(128)(4,1)S(1)}, s32[]{:S(2)}) async-start(s8[16777216]{0:T(1024)(128)(4,1)} %bitcast.46), calls=%async_computation.6 | async-start | bytes 8388608
  246.3 20.0 %slice-start.1 = ((s8[16777216]{0:T(1024)(128)(4,1)}), s8[4194304]{0:T(1024)(128)(4,1)S(1)}, s32[]{:S(2)}) async-start(s8[16777216]{0:T(1024)(128)(4,1)} %bitcast.46), calls=%async_computation.7 | async-start | bytes 8388608
  246.3 20.0 %slice-start.2 = ((s8[16777216]{0:T(1024)(128)(4,1)}), s8[4194304]{0:T(1024)(128)(4,1)S(1)}, s32[]{:S(2)}) async-start(s8[16777216]{0:T(1024)(128)(4,1)} %bitcast.46), calls=%async_computation.8 | async-start | bytes 8388608
  254.5 10.4 %copy-start = (bf16[16,1024,128]{2,1,0:T(8,128)(2,1)S(1)}, bf16[16,1024,128]{2,1,0:T(8,128)(2,1)}, u32[]{:S(2)}) copy-start(bf16[16,1024,128]{2,1,0:T(8,128)(2,1)} %param.14) | copy-start | bytes 12582916
  263.4 2.9 %slice-start.3 = ((s8[16777216]{0:T(1024)(128)(4,1)}), s8[4194304]{0:T(1024)(128)(4,1)S(1)}, s32[]{:S(2)}) async-start(s8[16777216]{0:T(1024)(128)(4,1)} %bitcast.46), calls=%async_computation.9 | async-start | bytes 8388608
Sparse Core Ops, SparseCore 0:
  12.0 35.2 reduce-scatter.1
  48.9 45.1 all-gather.4
  96.4 149.8 all-gather.2
where the time goes:
time: 280 us; the launch traced here: 279 us
  waiting for transfers between devices  123 us (44%)
  blocking collectives  65.9 us (24%)
  local copies, waits for them, and re-layouts  34.3 us (12%)
  other arithmetic  23.9 us (9%)
  matrix products  18 us (6%)
  between operations  14 us (5%)
    all_gather x1, waiting for transfers between devices, per_device(): lax.all_gather(flat_query, 'replica', axis=0, tiled=True)  123 us
    all_to_all x1, blocking collectives, per_device(): lax.all_to_all(query_rows, 'tp', split_axis=2, concat_axis=0, tiled=True)  27.9 us
    unnamed x2, other arithmetic  21.6 us
    unnamed x29, local copies, waits for them, and re-layouts  17.2 us
    all_to_all x1, blocking collectives, per_device(): lax.all_to_all(w_keyvalue, 'tp', split_axis=2, concat_axis=0, tiled=True)  13.5 us
    all_gather x1, blocking collectives, per_device(): lax.all_gather(query_local, 'tp', axis=1, tiled=True)  8.68 us
    all_gather x1, blocking collectives, per_device(): whole = lax.all_gather(embedded, 'tp', axis=1, tiled=True)  8.37 us
    dot_general x1, matrix products, per_device(): query_acc = jnp.dot(normed, query_full, preferred_element_type=jnp.float32)  8.22 us
  transfers between devices with their start and end apart: 3, of which 1 were waited for; matrix products, arithmetic and copies ran while one was open for 19% of the time, Pallas kernels for 0%

commit v1 on v0

--- a/solution.py
+++ b/solution.py
@@ -1,6 +1,10 @@
+import functools
+
 import jax
 import jax.numpy as jnp
 from jax import lax
+from jax.experimental import pallas as pl
+from jax.experimental.pallas import tpu as pltpu
 from jax.sharding import PartitionSpec as P
 
 
@@ -101,9 +105,409 @@
     return (context, query_full, pair_full.reshape(width, 2, pair_cols))
 
 
+MESH = pl.DeviceIdType.MESH
+
+
+def exchange_kernel(
+    planes,
+    part_ref,
+    gain_ref,
+    query_ref,
+    pair_ref,
+    query_out,
+    pair_out,
+    normed_ref,
+    spread_ref,
+    query_hold,
+    pair_hold,
+    picked,
+    pieces,
+    send_sem,
+    recv_sem,
+    plane_sem,
+    local_sem,
+    pick_send,
+    pick_recv,
+    piece_send,
+    piece_recv,
+):
+    r, t = lax.axis_index("replica"), lax.axis_index("tp")
+    replicas = 2 * planes
+    z, k = r // 2, lax.rem(r, 2)
+    ty, tx = t // 2, lax.rem(t, 2)
+    rows, query_cols = query_hold.shape
+    pair_cols = pair_hold.shape[2]
+    batch, feats = picked.shape[1], picked.shape[2]
+    other = [t, ty * 2 + 1 - tx, (1 - ty) * 2 + tx, 3 - t]
+    partner = z * 2 + 1 - k
+    width = replicas * 4 * rows
+
+    barrier = pltpu.get_barrier_semaphore()
+    for step in range(1, replicas):
+        pl.semaphore_signal(
+            barrier, inc=1, device_id=(lax.rem(r + step, replicas), t), device_id_type=MESH
+        )
+    for j in range(1, 4):
+        pl.semaphore_signal(barrier, inc=1, device_id=(r, other[j]), device_id_type=MESH)
+    pl.semaphore_wait(barrier, replicas - 1 + 3)
+
+    def piece_id(plane, core, tp):
+        return (plane * 2 + core) * 4 + tp
+
+    def rows_of(ref, pid):
+        where = pl.ds(pl.multiple_of(pid * rows, rows), rows)
+        return ref.at[where]
+
+    def columns(tp):
+        return (
+            query_ref.at[:, pl.ds(pl.multiple_of(tp * query_cols, query_cols), query_cols)],
+            pair_ref.at[:, :, pl.ds(pl.multiple_of(tp * pair_cols, pair_cols), pair_cols)],
+        )
+
+    def copies(pid, sources, way, slot, target):
+        made = []
+        for c, (source, out) in enumerate(zip(sources, (query_out, pair_out))):
+            sem = plane_sem.at[c, slot] if way is None else send_sem.at[c, way, slot]
+            made.append(
+                pltpu.make_async_remote_copy(
+                    src_ref=source,
+                    dst_ref=rows_of(out, pid),
+                    send_sem=sem,
+                    recv_sem=recv_sem.at[c, pid],
+                    device_id=target,
+                    device_id_type=MESH,
+                )
+            )
+        return made
+
+    def landed(pid):
+        for c, out in enumerate((query_out, pair_out)):
+            pltpu.make_async_copy(
+                rows_of(out, pid), rows_of(out, pid), recv_sem.at[c, pid]
+            ).wait()
+
+    def onward(pid, sources, slot, up, down, wait=False):
+        def act(made):
+            for copy in made:
+                copy.wait_send() if wait else copy.start()
+
+        if up:
+
+            @pl.when(z < planes - 1)
+            def _():
+                act(copies(pid, sources, 0, slot, (lax.rem(r + 2, replicas), t)))
+
+        if down:
+
+            @pl.when(z > 0)
+            def _():
+                act(copies(pid, sources, 1, slot, (lax.rem(r + replicas - 2, replicas), t)))
+
+        act(copies(pid, sources, 2, slot, (partner, t)))
+
+    def stored(pid):
+        return rows_of(query_out, pid), rows_of(pair_out, pid)
+
+    mine = piece_id(z, k, t)
+    sources = columns(t)
+    bring = [
+        pltpu.make_async_copy(sources[0], query_hold, local_sem.at[0]),
+        pltpu.make_async_copy(sources[1], pair_hold, local_sem.at[1]),
+    ]
+    across = [copies(mine, columns(other[j]), None, j - 1, (r, other[j])) for j in range(1, 4)]
+    for made in across:
+        for copy in made:
+            copy.start()
+    onward(mine, sources, 0, True, True)
+    for copy in bring:
+        copy.start()
+
+    def batch_rows(replica):
+        return part_ref.at[pl.ds(pl.multiple_of(replica * batch, batch), batch)]
+
+    keep = pltpu.make_async_copy(batch_rows(r), picked.at[r], local_sem.at[2])
+    keep.start()
+    picks = []
+    for step in range(1, replicas):
+        target = lax.rem(r + step, replicas)
+        picks.append(
+            pltpu.make_async_remote_copy(
+                src_ref=batch_rows(target),
+                dst_ref=picked.at[r],
+                send_sem=pick_send.at[step],
+                recv_sem=pick_recv.at[step],
+                device_id=(target, t),
+                device_id_type=MESH,
+            )
+        )
+    for copy in picks:
+        copy.start()
+    for copy in bring:
+        copy.wait()
+    put = [
+        pltpu.make_async_copy(query_hold, rows_of(query_out, mine), local_sem.at[3]),
+        pltpu.make_async_copy(pair_hold, rows_of(pair_out, mine), local_sem.at[4]),
+    ]
+    for copy in put:
+        copy.start()
+
+    gather = [
+        pltpu.make_async_remote_copy(
+            src_ref=pieces.at[t],
+            dst_ref=pieces.at[t],
+            send_sem=piece_send.at[j - 1],
+            recv_sem=piece_recv.at[j - 1],
+            device_id=(r, other[j]),
+            device_id_type=MESH,
+        )
+        for j in range(1, 4)
+    ]
+
+    def sum_picks():
+        keep.wait()
+        for copy in picks:
+            copy.wait()
+        total = picked[0].astype(jnp.float32)
+        for step in range(1, replicas):
+            total = total + picked[step].astype(jnp.float32)
+        pieces[t] = total.astype(jnp.bfloat16)
+
+    def normalise():
+        for copy in gather:
+            copy.wait()
+        square = jnp.zeros((batch, 1), jnp.float32)
+        for i in range(4):
+            part = pieces[i].astype(jnp.float32)
+            square = square + jnp.sum(part * part, axis=1, keepdims=True)
+        factor = lax.rsqrt(square / (4 * feats) + 1e-05)
+        for i in range(4):
+            part = pieces[i].astype(jnp.float32)
+            gain = gain_ref[:, i * feats : (i + 1) * feats].astype(jnp.float32)
+            normed_ref[:, i * feats : (i + 1) * feats] = (part * factor * gain).astype(
+                jnp.bfloat16
+            )
+        block = 256
+        line = lax.broadcasted_iota(jnp.int32, (block, 2 * block), 0)
+        column = lax.broadcasted_iota(jnp.int32, (block, 2 * block), 1)
+        even = (column == 2 * line).astype(jnp.bfloat16)
+        odd = (column == 2 * line + 1).astype(jnp.bfloat16)
+
+        def spread(i, carry):
+            part = normed_ref[:, pl.ds(pl.multiple_of(i * block, block), block)]
+            where = pl.ds(pl.multiple_of(i * 2 * block, 2 * block), 2 * block)
+            spread_ref[0:batch, where] = jnp.dot(
+                part, even, preferred_element_type=jnp.float32
+            ).astype(jnp.bfloat16)
+            spread_ref[batch : 2 * batch, where] = jnp.dot(
+                part, odd, preferred_element_type=jnp.float32
+            ).astype(jnp.bfloat16)
+            return carry
+
+        lax.fori_loop(0, 4 * feats // block, spread, 0)
+
+    steps = 4 * (planes - 1)
+    for step in range(steps):
+        if 0 < step < 4:
+            pid = piece_id(z, k, other[step])
+            landed(pid)
+            onward(pid, stored(pid), step, True, True)
+        far, j = step // 4 + 1, step % 4
+
+        @pl.when(z >= far)
+        def _():
+            pid = piece_id(lax.rem(z + planes - far, planes), k, other[j])
+            landed(pid)
+            onward(pid, stored(pid), 4 * far + j, True, False)
+
+        @pl.when(z + far < planes)
+        def _():
+            pid = piece_id(lax.rem(z + far, planes), k, other[j])
+            landed(pid)
+            onward(pid, stored(pid), 4 * (planes - 1 + far) + j, False, True)
+
+        if step == 5:
+            sum_picks()
+        if step == 7:
+            for copy in gather:
+                copy.start()
+        if step == 8:
+            normalise()
+
+    for copy in put:
+        copy.wait()
+    for made in across:
+        for copy in made:
+            copy.wait_send()
+    onward(mine, sources, 0, True, True, wait=True)
+    for j in range(1, 4):
+        pid = piece_id(z, k, other[j])
+        onward(pid, stored(pid), j, True, True, wait=True)
+    for step in range(steps):
+        far, j = step // 4 + 1, step % 4
+
+        @pl.when(z >= far)
+        def _():
+            pid = piece_id(lax.rem(z + planes - far, planes), k, other[j])
+            onward(pid, stored(pid), 4 * far + j, True, False, wait=True)
+
+        @pl.when(z + far < planes)
+        def _():
+            pid = piece_id(lax.rem(z + far, planes), k, other[j])
+            onward(pid, stored(pid), 4 * (planes - 1 + far) + j, False, True, wait=True)
+
+    for plane in range(planes):
+        for j in range(4):
+            landed(piece_id(plane, 1 - k, j))
+
+
+def exchange(part, norm_gain, w_query, w_keyvalue, planes, batch):
+    rows, all_query = w_query.shape
+    query_cols, pair_cols = all_query // 4, w_keyvalue.shape[2] // 4
+    replicas = 2 * planes
+    width = rows * replicas * 4
+    feats = part.shape[1]
+    anywhere = pl.BlockSpec(memory_space=pl.ANY)
+    vmem = pl.BlockSpec(memory_space=pltpu.VMEM)
+    dma = pltpu.SemaphoreType.DMA
+    slots = 4 * (2 * planes - 1)
+    return pl.pallas_call(
+        functools.partial(exchange_kernel, planes),
+        out_shape=(
+            jax.ShapeDtypeStruct((width, query_cols), w_query.dtype),
+            jax.ShapeDtypeStruct((width, 2, pair_cols), w_query.dtype),
+            jax.ShapeDtypeStruct((batch, width), w_query.dtype),
+            jax.ShapeDtypeStruct((2 * batch, 2 * width), w_query.dtype),
+        ),
+        in_specs=[anywhere, vmem, anywhere, anywhere],
+        out_specs=(anywhere, anywhere, vmem, vmem),
+        scratch_shapes=[
+            pltpu.VMEM((rows, query_cols), w_query.dtype),
+            pltpu.VMEM((rows, 2, pair_cols), w_query.dtype),
+            pltpu.VMEM((replicas, batch, feats), part.dtype),
+            pltpu.VMEM((4, batch, feats), part.dtype),
+            dma((2, 3, slots)),
+            dma((2, replicas * 4)),
+            dma((2, 3)),
+            dma((5,)),
+            dma((replicas,)),
+            dma((replicas,)),
+            dma((3,)),
+            dma((3,)),
+        ],
+        compiler_params=pltpu.CompilerParams(
+            collective_id=0, has_side_effects=True, vmem_limit_bytes=12 * 2**20
+        ),
+        cost_estimate=pl.CostEstimate(
+            flops=2 * 10**11, bytes_accessed=2 * width * query_cols, transcendentals=0
+        ),
+        name="weight_exchange",
+    )(part, norm_gain.reshape(1, -1), w_query, w_keyvalue)
+
+
+def project_kernel(
+    normed_ref, spread_ref, query_in, pair_in, query_ref, pair_ref, q_ref, kv_ref, q_acc, kv_acc
+):
+    step = pl.program_id(0)
+
+    @pl.when(step == 0)
+    def _():
+        q_acc[...] = jnp.zeros_like(q_acc)
+        kv_acc[...] = jnp.zeros_like(kv_acc)
+
+    query_ref[...] = query_in[...]
+    pair_ref[...] = pair_in[...]
+    q_acc[...] += jnp.dot(normed_ref[...], query_in[...], preferred_element_type=jnp.float32)
+    kv_acc[...] += jnp.dot(spread_ref[...], pair_in[...], preferred_element_type=jnp.float32)
+
+    @pl.when(step == pl.num_programs(0) - 1)
+    def _():
+        q_ref[...] = q_acc[...].astype(q_ref.dtype)
+        kv_ref[...] = kv_acc[...].astype(kv_ref.dtype)
+
+
+def project(normed, spread, query_all, pair_all):
+    batch, width = normed.shape
+    query_cols, pair_cols = query_all.shape[1], pair_all.shape[2]
+    pair_flat = pair_all.reshape(2 * width, pair_cols)
+    block = 512
+    query_spec = pl.BlockSpec((block, query_cols), lambda i: (i, 0))
+    pair_spec = pl.BlockSpec((2 * block, pair_cols), lambda i: (i, 0))
+    query_out, pair_out, query, pair = pl.pallas_call(
+        project_kernel,
+        grid=(width // block,),
+        out_shape=(
+            jax.ShapeDtypeStruct(query_all.shape, query_all.dtype),
+            jax.ShapeDtypeStruct(pair_flat.shape, pair_all.dtype),
+            jax.ShapeDtypeStruct((batch, query_cols), normed.dtype),
+            jax.ShapeDtypeStruct((2 * batch, pair_cols), normed.dtype),
+        ),
+        in_specs=[
+            pl.BlockSpec((batch, block), lambda i: (0, i)),
+            pl.BlockSpec((2 * batch, 2 * block), lambda i: (0, i)),
+            query_spec,
+            pair_spec,
+        ],
+        out_specs=(
+            query_spec,
+            pair_spec,
+            pl.BlockSpec((batch, query_cols), lambda i: (0, 0)),
+            pl.BlockSpec((2 * batch, pair_cols), lambda i: (0, 0)),
+        ),
+        scratch_shapes=[
+            pltpu.VMEM((batch, query_cols), jnp.float32),
+            pltpu.VMEM((2 * batch, pair_cols), jnp.float32),
+        ],
+        compiler_params=pltpu.CompilerParams(vmem_limit_bytes=16 * 2**20),
+        cost_estimate=pl.CostEstimate(
+            flops=2 * batch * width * (query_cols + 4 * pair_cols),
+            bytes_accessed=4 * width * (query_cols + 2 * pair_cols),
+            transcendentals=0,
+        ),
+        name="project_and_store",
+    )(normed, spread, query_all, pair_flat)
+    return query_out, pair_out.reshape(width, 2, pair_cols), query, pair
+
+
+def per_device_line(
+    planes,
+    token_ids,
+    embed_table,
+    norm_gain,
+    w_query,
+    w_keyvalue,
+    key_cache,
+    value_cache,
+    cache_lengths,
+):
+    vocab_rows = embed_table.shape[0]
+    batch = cache_lengths.shape[0]
+    head_size = key_cache.shape[2]
+    picked = token_ids - lax.axis_index("replica") * vocab_rows
+    columns = lax.broadcasted_iota(jnp.int32, (token_ids.shape[0], vocab_rows), 1)
+    onehot = (picked[:, None] == columns).astype(jnp.bfloat16)
+    part = jnp.dot(onehot, embed_table, preferred_element_type=jnp.float32).astype(jnp.bfloat16)
+    query_all, pair_all, normed, spread = exchange(
+        part, norm_gain, w_query, w_keyvalue, planes, batch
+    )
+    query_out, pair_out, query, pair = project(normed, spread, query_all, pair_all)
+    query = query.reshape(batch, -1, head_size)
+    context = attend(query, key_cache, value_cache, pair[:batch], pair[batch:], cache_lengths)
+    return context.reshape(batch, -1), query_out, pair_out
+
+
 def solution(mesh):
+    replicas, tp = mesh.shape["replica"], mesh.shape["tp"]
+
+    def body(*args):
+        key_cache, lengths, w_keyvalue = args[5], args[7], args[4]
+        one_head = w_keyvalue.shape[2] == tp * key_cache.shape[2]
+        own_rows = key_cache.shape[0] == lengths.shape[0]
+        if tp == 4 and replicas % 2 == 0 and replicas > 6 and one_head and own_rows:
+            return per_device_line(replicas // 2, *args)
+        return per_device(*args)
+
     return jax.shard_map(
-        per_device,
+        body,
         mesh=mesh,
         in_specs=(
             P(),

time: 280 us -> 213 us (0.76)
  Pallas kernels: 0 us -> 204 us
  waiting for transfers between devices: 123 us -> 0 us
  blocking collectives: 65.9 us -> 0 us
  local copies, waits for them, and re-layouts: 34.3 us -> 1.88 us
  other arithmetic: 23.9 us -> 1.07 us
  between operations: 14 us -> 0.73 us
  matrix products: 18 us -> 5.06 us
    pallas_call x0 -> x2, Pallas kernels: none -> 204 us  [the longest x1 192 us: exchange(): pl.pallas_call(functools.partial(exchange_kernel, planes), out_shape=(jax...]
    all_gather x2 -> x0, waiting for transfers between devices: 123 us -> none  [the longest x1 123 us: per_device(): lax.all_gather(flat_query, 'replica', axis=0, tiled=True)]
    all_to_all x2 -> x0, blocking collectives: 41.4 us -> none  [the longest x1 27.9 us: per_device(): lax.all_to_all(query_rows, 'tp', split_axis=2, concat_axis=0, tiled=True)]
    all_gather x3 -> x0, blocking collectives: 24.5 us -> none  [the longest x1 8.68 us: per_device(): lax.all_gather(query_local, 'tp', axis=1, tiled=True)]
    unnamed x2 -> x0, other arithmetic: 21.6 us -> none
    unnamed x29 -> x12, local copies, waits for them, and re-layouts: 17.2 us -> 1.15 us
    reshape x3 -> x1, local copies, waits for them, and re-layouts: 14 us -> 0.74 us  [exchange(): norm_gain.reshape(1, -1)]
    dot_general x3 -> x1, matrix products: 15.9 us -> 2.95 us  [per_device_line(): jnp.dot(onehot, embed_table, preferred_element_type=jnp.float32)]
  transfers between devices with their start and end apart: 3 -> 0, of which waited for: 1 -> 0; matrix products, arithmetic and copies ran while one was open for 19% -> 0% of each run, Pallas kernels for 0% -> 0%
where the time goes in v1:
time: 213 us
  Pallas kernels  204 us (96%)
  matrix products  5.06 us (2%)
    pallas_call x1, Pallas kernels, exchange(): pl.pallas_call(functools.partial(exchange_kernel, planes), out_shape=(jax...  192 us
    pallas_call x1, Pallas kernels, project(): pl.pallas_call(project_kernel, grid=(width // block,), out_shape=(jax.Sha...  11.8 us

profile of v1, /device:TPU:0, one launch (start us, length us, event | category | flops | bytes accessed | tf_op | source)
XLA Modules:
  0.0 212.9 jit_solution(768331004905565198)
XLA Ops:
  0.6 0.0 copy-start.1
  0.6 0.0 copy-start
  0.7 0.8 broadcast_subtract_fusion
  1.5 0.7 reshape.27.gain_ref
  2.2 2.9 %convolution_convert_fusion.part_ref = bf16[128,2048]{1,0:T(8,128)(2,1)S(1)} fusion(bf16[1024,2048]{1,0:T(8,128)(2,1)} %param.9, s32[128]{0:T(128)S(1)} %broadcast_subtract_fusion), kind=kOutput, calls=%fused_computation | convolution fusion | flops 537264128 | bytes 4719104 | tf_op jit(solution)/shard_map/dot_general | solution.py:488
  5.2 0.0 copy-done.1
  5.2 0.0 copy-done
  5.2 192.4 %weight_exchange.1 = (bf16[8192,1024]{1,0:T(8,128)(2,1)S(1)}, bf16[8192,2,128]{2,1,0:T(2,128)(2,1)S(1)}, bf16[16,8192]{1,0:T(8,128)(2,1)S(1)}, bf16[32,16384]{1,0:T(8,128)(2,1)S(1)}) custom-call(bf16[128,2048]{1,0:T(8,128)(2,1)S(1)} %convolution_convert_fusion.part_ref, bf16[1,8192]{1,0:T(2,128)(2,1)S(1)} %reshape.27.gain_ref, ...), custom_call_target="tpu_custom_call" | custom-call | flops 199999995904 | bytes 16777216 | tf_op jit(solution)/shard_map/weight_exchange/pallas_call | solution.py:373
  197.5 0.0 copy-start.2
  197.6 0.0 copy-start.4
  197.6 11.8 %project_and_store.1 = (bf16[8192,1024]{1,0:T(8,128)(2,1)}, bf16[16384,128]{1,0:T(8,128)(2,1)}, bf16[16,1024]{1,0:T(8,128)(2,1)S(1)}, bf16[32,128]{1,0:T(8,128)(2,1)S(1)}) custom-call(bf16[16,8192]{1,0:T(8,128)(2,1)S(1)} %get-tuple-element.11.normed_ref, bf16[32,16384]{1,0:T(8,128)(2,1)S(1)} %get-tuple-element.12.spread_ref, ...), custom_call_target="tpu_custom_call" | custom-call | flops 402653184 | bytes 41943040 | tf_op jit(solution)/shard_map/project_and_store/pallas_call | solution.py:435
  209.3 0.0 copy-start.3
  209.4 0.1 fusion.6
  209.5 0.0 copy-done.2
  209.5 0.0 copy-done.4
  209.5 1.3 fusion.10
  210.8 0.2 fusion.2
  211.0 0.5 copy-done.3
  211.5 0.7 fusion.1
  212.2 0.6 copy.18
  (4 shorter events, 0.0 us)
Async XLA Ops:
  0.6 4.5 %copy-start.1 = (bf16[256,2,512]{2,1,0:T(2,128)(2,1)S(1)}, bf16[256,2,512]{2,1,0:T(2,128)(2,1)}, u32[]{:S(2)}) copy-start(bf16[256,2,512]{2,1,0:T(2,128)(2,1)} %pair_ref.1) | copy-start | bytes 1572868
  0.6 4.5 %copy-start = (bf16[256,4096]{1,0:T(8,128)(2,1)S(1)}, bf16[256,4096]{1,0:T(8,128)(2,1)}, u32[]{:S(2)}) copy-start(bf16[256,4096]{1,0:T(8,128)(2,1)} %query_ref.1) | copy-start | bytes 6291460
  197.5 11.9 %copy-start.2 = (bf16[16,1024,128]{2,1,0:T(8,128)(2,1)S(1)}, bf16[16,1024,128]{2,1,0:T(8,128)(2,1)}, u32[]{:S(2)}) copy-start(bf16[16,1024,128]{2,1,0:T(8,128)(2,1)} %param.13) | copy-start | bytes 12582916
  197.6 11.9 %copy-start.4 = (s32[16]{0:T(128)S(1)}, s32[16]{0:T(128)}, u32[]{:S(2)}) copy-start(s32[16]{0:T(128)} %param.15) | copy-start | bytes 196
  209.3 2.2 %copy-start.3 = (bf16[16,1024,128]{2,1,0:T(8,128)(2,1)S(1)}, bf16[16,1024,128]{2,1,0:T(8,128)(2,1)}, u32[]{:S(2)}) copy-start(bf16[16,1024,128]{2,1,0:T(8,128)(2,1)} %param.14) | copy-start | bytes 12582916

commit v2 on v1

--- a/solution.py
+++ b/solution.py
@@ -110,8 +110,9 @@
 
 def exchange_kernel(
     planes,
-    part_ref,
+    token_ref,
     gain_ref,
+    table_ref,
     query_ref,
     pair_ref,
     query_out,
@@ -120,12 +121,18 @@
     spread_ref,
     query_hold,
     pair_hold,
+    table_hold,
+    part_ref,
+    given,
+    joined,
     picked,
     pieces,
     send_sem,
     recv_sem,
     plane_sem,
     local_sem,
+    give_send,
+    give_recv,
     pick_send,
     pick_recv,
     piece_send,
@@ -222,26 +229,32 @@
     for copy in bring:
         copy.start()
 
-    def batch_rows(replica):
-        return part_ref.at[pl.ds(pl.multiple_of(replica * batch, batch), batch)]
-
-    keep = pltpu.make_async_copy(batch_rows(r), picked.at[r], local_sem.at[2])
-    keep.start()
+    table = pltpu.make_async_copy(table_ref, table_hold, local_sem.at[2])
+    table.start()
+    gives = [
+        pltpu.make_async_remote_copy(
+            src_ref=part_ref.at[plane, 1 - k],
+            dst_ref=given.at[plane],
+            send_sem=give_send.at[plane],
+            recv_sem=give_recv.at[plane],
+            device_id=(partner, t),
+            device_id_type=MESH,
+        )
+        for plane in range(planes)
+    ]
     picks = []
-    for step in range(1, replicas):
-        target = lax.rem(r + step, replicas)
+    for far in range(1, planes):
+        plane = lax.rem(z + far, planes)
         picks.append(
             pltpu.make_async_remote_copy(
-                src_ref=batch_rows(target),
-                dst_ref=picked.at[r],
-                send_sem=pick_send.at[step],
-                recv_sem=pick_recv.at[step],
-                device_id=(target, t),
+                src_ref=joined.at[plane],
+                dst_ref=picked.at[far - 1],
+                send_sem=pick_send.at[far - 1],
+                recv_sem=pick_recv.at[far - 1],
+                device_id=(plane * 2 + k, t),
                 device_id_type=MESH,
             )
         )
-    for copy in picks:
-        copy.start()
     for copy in bring:
         copy.wait()
     put = [
@@ -263,13 +276,37 @@
         for j in range(1, 4)
     ]
 
+    def select_rows():
+        table.wait()
+        vocab_rows = table_hold.shape[0]
+        tokens = token_ref.shape[0]
+        columns = lax.broadcasted_iota(jnp.int32, (tokens, vocab_rows), 1)
+        onehot = (token_ref[...] - r * vocab_rows == columns).astype(jnp.bfloat16)
+        block = 256
+
+        def select(i, carry):
+            where = pl.ds(pl.multiple_of(i * block, block), block)
+            rows_here = jnp.dot(
+                onehot, table_hold[:, where], preferred_element_type=jnp.float32
+            ).astype(jnp.bfloat16)
+            part_ref[:, :, :, where] = rows_here.reshape(planes, 2, batch, block)
+            return carry
+
+        lax.fori_loop(0, feats // block, select, 0)
+
+    def join():
+        for copy in gives:
+            copy.wait()
+        for plane in range(planes):
+            own = part_ref[plane, k].astype(jnp.float32)
+            joined[plane] = (own + given[plane].astype(jnp.float32)).astype(jnp.bfloat16)
+
     def sum_picks():
-        keep.wait()
         for copy in picks:
             copy.wait()
-        total = picked[0].astype(jnp.float32)
-        for step in range(1, replicas):
-            total = total + picked[step].astype(jnp.float32)
+        total = joined[z].astype(jnp.float32)
+        for far in range(1, planes):
+            total = total + picked[far - 1].astype(jnp.float32)
         pieces[t] = total.astype(jnp.bfloat16)
 
     def normalise():
@@ -325,12 +362,22 @@
             landed(pid)
             onward(pid, stored(pid), 4 * (planes - 1 + far) + j, False, True)
 
-        if step == 5:
+        if step == 0:
+            select_rows()
+        if step == 1:
+            for copy in gives:
+                copy.start()
+        if step == 2:
+            join()
+        if step == 3:
+            for copy in picks:
+                copy.start()
+        if step == 7:
             sum_picks()
-        if step == 7:
+        if step == 8:
             for copy in gather:
                 copy.start()
-        if step == 8:
+        if step == 9:
             normalise()
 
     for copy in put:
@@ -360,14 +407,16 @@
             landed(piece_id(plane, 1 - k, j))
 
 
-def exchange(part, norm_gain, w_query, w_keyvalue, planes, batch):
+def exchange(token_ids, norm_gain, embed_table, w_query, w_keyvalue, planes, batch):
     rows, all_query = w_query.shape
     query_cols, pair_cols = all_query // 4, w_keyvalue.shape[2] // 4
     replicas = 2 * planes
     width = rows * replicas * 4
-    feats = part.shape[1]
+    feats = embed_table.shape[1]
+    kind = w_query.dtype
     anywhere = pl.BlockSpec(memory_space=pl.ANY)
     vmem = pl.BlockSpec(memory_space=pltpu.VMEM)
+    hbm = pl.BlockSpec(memory_space=pltpu.HBM)
     dma = pltpu.SemaphoreType.DMA
     slots = 4 * (2 * planes - 1)
     return pl.pallas_call(
@@ -378,44 +427,66 @@
             jax.ShapeDtypeStruct((batch, width), w_query.dtype),
             jax.ShapeDtypeStruct((2 * batch, 2 * width), w_query.dtype),
         ),
-        in_specs=[anywhere, vmem, anywhere, anywhere],
+        in_specs=[vmem, vmem, hbm, hbm, hbm],
         out_specs=(anywhere, anywhere, vmem, vmem),
         scratch_shapes=[
             pltpu.VMEM((rows, query_cols), w_query.dtype),
             pltpu.VMEM((rows, 2, pair_cols), w_query.dtype),
-            pltpu.VMEM((replicas, batch, feats), part.dtype),
-            pltpu.VMEM((4, batch, feats), part.dtype),
+            pltpu.VMEM(embed_table.shape, kind),
+            pltpu.VMEM((planes, 2, batch, feats), kind),
+            pltpu.VMEM((planes, batch, feats), kind),
+            pltpu.VMEM((planes, batch, feats), kind),
+            pltpu.VMEM((planes - 1, batch, feats), kind),
+            pltpu.VMEM((4, batch, feats), kind),
             dma((2, 3, slots)),
             dma((2, replicas * 4)),
             dma((2, 3)),
             dma((5,)),
-            dma((replicas,)),
-            dma((replicas,)),
+            dma((planes,)),
+            dma((planes,)),
+            dma((planes - 1,)),
+            dma((planes - 1,)),
             dma((3,)),
             dma((3,)),
         ],
         compiler_params=pltpu.CompilerParams(
-            collective_id=0, has_side_effects=True, vmem_limit_bytes=12 * 2**20
+            collective_id=0, has_side_effects=True, vmem_limit_bytes=20 * 2**20
         ),
         cost_estimate=pl.CostEstimate(
             flops=2 * 10**11, bytes_accessed=2 * width * query_cols, transcendentals=0
         ),
         name="weight_exchange",
-    )(part, norm_gain.reshape(1, -1), w_query, w_keyvalue)
+    )(token_ids.reshape(-1, 1), norm_gain.reshape(1, -1), embed_table, w_query, w_keyvalue)
 
 
 def project_kernel(
-    normed_ref, spread_ref, query_in, pair_in, query_ref, pair_ref, q_ref, kv_ref, q_acc, kv_acc
+    normed_ref,
+    spread_ref,
+    query_in,
+    pair_in,
+    query_all,
+    pair_all,
+    query_ref,
+    pair_ref,
+    q_ref,
+    kv_ref,
+    q_acc,
+    kv_acc,
+    sems,
 ):
     step = pl.program_id(0)
+    stores = [
+        pltpu.make_async_copy(query_all, query_ref, sems.at[0]),
+        pltpu.make_async_copy(pair_all, pair_ref, sems.at[1]),
+    ]
 
     @pl.when(step == 0)
     def _():
+        for copy in stores:
+            copy.start()
         q_acc[...] = jnp.zeros_like(q_acc)
         kv_acc[...] = jnp.zeros_like(kv_acc)
 
-    query_ref[...] = query_in[...]
-    pair_ref[...] = pair_in[...]
     q_acc[...] += jnp.dot(normed_ref[...], query_in[...], preferred_element_type=jnp.float32)
     kv_acc[...] += jnp.dot(spread_ref[...], pair_in[...], preferred_element_type=jnp.float32)
 
@@ -423,6 +494,8 @@
     def _():
         q_ref[...] = q_acc[...].astype(q_ref.dtype)
         kv_ref[...] = kv_acc[...].astype(kv_ref.dtype)
+        for copy in stores:
+            copy.wait()
 
 
 def project(normed, spread, query_all, pair_all):
@@ -430,6 +503,8 @@
     query_cols, pair_cols = query_all.shape[1], pair_all.shape[2]
     pair_flat = pair_all.reshape(2 * width, pair_cols)
     block = 512
+    anywhere = pl.BlockSpec(memory_space=pl.ANY)
+    hbm = pl.BlockSpec(memory_space=pltpu.HBM)
     query_spec = pl.BlockSpec((block, query_cols), lambda i: (i, 0))
     pair_spec = pl.BlockSpec((2 * block, pair_cols), lambda i: (i, 0))
     query_out, pair_out, query, pair = pl.pallas_call(
@@ -446,16 +521,19 @@
             pl.BlockSpec((2 * batch, 2 * block), lambda i: (0, i)),
             query_spec,
             pair_spec,
+            anywhere,
+            anywhere,
         ],
         out_specs=(
-            query_spec,
-            pair_spec,
+            hbm,
+            hbm,
             pl.BlockSpec((batch, query_cols), lambda i: (0, 0)),
             pl.BlockSpec((2 * batch, pair_cols), lambda i: (0, 0)),
         ),
         scratch_shapes=[
             pltpu.VMEM((batch, query_cols), jnp.float32),
             pltpu.VMEM((2 * batch, pair_cols), jnp.float32),
+            pltpu.SemaphoreType.DMA((2,)),
         ],
         compiler_params=pltpu.CompilerParams(vmem_limit_bytes=16 * 2**20),
         cost_estimate=pl.CostEstimate(
@@ -464,7 +542,7 @@
             transcendentals=0,
         ),
         name="project_and_store",
-    )(normed, spread, query_all, pair_flat)
+    )(normed, spread, query_all, pair_flat, query_all, pair_flat)
     return query_out, pair_out.reshape(width, 2, pair_cols), query, pair
 
 
@@ -479,15 +557,10 @@
     value_cache,
     cache_lengths,
 ):
-    vocab_rows = embed_table.shape[0]
     batch = cache_lengths.shape[0]
     head_size = key_cache.shape[2]
-    picked = token_ids - lax.axis_index("replica") * vocab_rows
-    columns = lax.broadcasted_iota(jnp.int32, (token_ids.shape[0], vocab_rows), 1)
-    onehot = (picked[:, None] == columns).astype(jnp.bfloat16)
-    part = jnp.dot(onehot, embed_table, preferred_element_type=jnp.float32).astype(jnp.bfloat16)
     query_all, pair_all, normed, spread = exchange(
-        part, norm_gain, w_query, w_keyvalue, planes, batch
+        token_ids, norm_gain, embed_table, w_query, w_keyvalue, planes, batch
     )
     query_out, pair_out, query, pair = project(normed, spread, query_all, pair_all)
     query = query.reshape(batch, -1, head_size)

time: 213 us -> 205 us (0.962)
  Pallas kernels: 204 us -> 194 us
  local copies, waits for them, and re-layouts: 1.88 us -> 7.45 us
  matrix products: 5.06 us -> 2.12 us
    pallas_call x1, Pallas kernels: 192 us -> 185 us  [exchange(): pl.pallas_call(functools.partial(exchange_kernel, planes), out_shape=(jax...]
    unnamed x12 -> x14, local copies, waits for them, and re-layouts: 1.15 us -> 5.94 us
    pallas_call x1, Pallas kernels: 11.8 us -> 8.32 us  [project(): pl.pallas_call(project_kernel, grid=(width // block,), out_shape=(jax.Sha...]
    dot_general x1 -> x0, matrix products: 2.95 us -> none  [per_device_line(): jnp.dot(onehot, embed_table, preferred_element_type=jnp.float32)]
where the time goes in v2:
time: 205 us; the launch traced here: 204 us
  Pallas kernels  194 us (95%)
  local copies, waits for them, and re-layouts  7.45 us (4%)
  matrix products  2.12 us (1%)
    pallas_call x1, Pallas kernels, exchange(): pl.pallas_call(functools.partial(exchange_kernel, planes), out_shape=(jax...  185 us
    pallas_call x1, Pallas kernels, project(): pl.pallas_call(project_kernel, grid=(width // block,), out_shape=(jax.Sha...  8.32 us
    unnamed x14, local copies, waits for them, and re-layouts  5.94 us

profile of v2, /device:TPU:0, one launch (start us, length us, event | category | flops | bytes accessed | tf_op | source)
XLA Modules:
  0.0 204.2 jit_solution(8519001430999846309)
XLA Ops:
  0.6 0.7 reshape.30.gain_ref
  1.4 0.8 copy.11.token_ref
  2.1 0.0 copy-start
  2.1 2.2 %copy-done = bf16[1024,2048]{1,0:T(8,128)(2,1)S(1)} copy-done((bf16[1024,2048]{1,0:T(8,128)(2,1)S(1)}, bf16[1024,2048]{1,0:T(8,128)(2,1)}, u32[]{:S(2)}) %copy-start) | copy-done | bytes 4194328
  4.3 0.0 copy-start.1
  4.3 1.6 copy-done.1
  5.9 0.0 copy-start.2
  5.9 1.0 copy-done.2
  7.0 185.3 %weight_exchange.1 = (bf16[8192,1024]{1,0:T(8,128)(2,1)S(1)}, bf16[8192,2,128]{2,1,0:T(2,128)(2,1)S(1)}, bf16[16,8192]{1,0:T(8,128)(2,1)S(1)}, bf16[32,16384]{1,0:T(8,128)(2,1)S(1)}) custom-call(s32[128,1]{1,0:T(8,128)S(1)} %copy.11.token_ref, bf16[1,8192]{1,0:T(2,128)(2,1)S(1)} %reshape.30.gain_ref, bf16[1024,2048]{1,0:T(8,128)(2,1)S(1)} %copy-done, ...), custom_call_target="tpu_custom_call" | custom-call | flops 199999995904 | bytes 16777216 | tf_op jit(solution)/shard_map/weight_exchange/pallas_call | solution.py:422
  192.3 0.0 copy-start.3
  192.3 0.0 copy-start.5
  192.3 8.3 %project_and_store.1 = (bf16[8192,1024]{1,0:T(8,128)(2,1)}, bf16[16384,128]{1,0:T(8,128)(2,1)}, bf16[16,1024]{1,0:T(8,128)(2,1)S(1)}, bf16[32,128]{1,0:T(8,128)(2,1)S(1)}) custom-call(bf16[16,8192]{1,0:T(8,128)(2,1)S(1)} %get-tuple-element.11.normed_ref, bf16[32,16384]{1,0:T(8,128)(2,1)S(1)} %get-tuple-element.12.spread_ref, ...), custom_call_target="tpu_custom_call" | custom-call | flops 402653184 | bytes 41943040 | tf_op jit(solution)/shard_map/project_and_store/pallas_call | solution.py:510
  200.6 0.0 copy-start.4
  200.7 0.1 fusion.5
  200.8 0.0 copy-done.3
  200.8 0.0 copy-done.5
  200.8 1.3 fusion.9
  202.1 0.2 fusion.2
  202.4 0.5 copy-done.4
  202.8 0.7 fusion.1
  203.6 0.6 copy.19
  (4 shorter events, 0.0 us)
Async XLA Ops:
  2.1 2.2 %copy-start = (bf16[1024,2048]{1,0:T(8,128)(2,1)S(1)}, bf16[1024,2048]{1,0:T(8,128)(2,1)}, u32[]{:S(2)}) copy-start(bf16[1024,2048]{1,0:T(8,128)(2,1)} %table_ref.1) | copy-start | bytes 12582916
  4.3 1.6 copy-start.1
  5.9 1.0 copy-start.2
  192.3 8.5 %copy-start.3 = (bf16[16,1024,128]{2,1,0:T(8,128)(2,1)S(1)}, bf16[16,1024,128]{2,1,0:T(8,128)(2,1)}, u32[]{:S(2)}) copy-start(bf16[16,1024,128]{2,1,0:T(8,128)(2,1)} %param.13) | copy-start | bytes 12582916
  192.3 8.5 %copy-start.5 = (s32[16]{0:T(128)S(1)}, s32[16]{0:T(128)}, u32[]{:S(2)}) copy-start(s32[16]{0:T(128)} %param.15) | copy-start | bytes 196
  200.6 2.2 %copy-start.4 = (bf16[16,1024,128]{2,1,0:T(8,128)(2,1)S(1)}, bf16[16,1024,128]{2,1,0:T(8,128)(2,1)}, u32[]{:S(2)}) copy-start(bf16[16,1024,128]{2,1,0:T(8,128)(2,1)} %param.14) | copy-start | bytes 12582916
